TPU v7x, 256 devices: a whole 4x4x8 slice. The times are simulated.
256 devices in a mesh: zero: 8 (over z_hi, core), model: 32 (over z_lo, y, x).
Axes of the slice: x: 4, y: 4, z: 8 (z_hi: 4, z_lo: 2; z = z_hi * 2 + z_lo), core: 2. Of those that a mesh axis runs over, the one named last changes fastest.
Arguments:
- w_gate: float32 [5120, 13824], P('zero', 'model'), may hold values from -0.15625 to 0.15625
- first_gate: float32 [5120, 13824], P('zero', 'model'), may hold values from -0.078125 to 0.078125
- second_gate: float32 [5120, 13824], P('zero', 'model'), may hold values from -0.078125 to 0.078125
- w_up: float32 [5120, 13824], P('zero', 'model'), may hold values from -0.15625 to 0.15625
- first_up: float32 [5120, 13824], P('zero', 'model'), may hold values from -0.078125 to 0.078125
- second_up: float32 [5120, 13824], P('zero', 'model'), may hold values from -0.078125 to 0.078125
- norm_train: float32 [5120], P(('zero', 'model')), may hold values from 0.25 to 1.75
- norm_step: float32 [5120], P(('zero', 'model')), may hold values from -0.3 to 0.3
Outputs:
- ready_gate: bfloat16 [5120, 13824], P(None, 'model')
- ready_up: bfloat16 [5120, 13824], P(None, 'model')
- column_gate: float32 [13824], P('model')
- column_up: float32 [13824], P('model')
- serve_norm: bfloat16 [5120], replicated
- latest_gate: float32 [5120, 13824], P('zero', 'model')
- latest_up: float32 [5120, 13824], P('zero', 'model')
All inputs are finite; a program needn't handle non-finite values. Where the computation divides by a largest or mean magnitude, that divisor is 1e-20 or more.
Results may differ from a plain program's by a relative error of at most 0.001.
Values may be sent and summed in bfloat16 or wider, within the bound.
A program may use at most 128 MiB of HBM per device.

v0:
```python
import jax
import jax.numpy as jnp
from jax import lax
from jax.sharding import PartitionSpec as P

learn_rate = 0.25
hold_rate = 0.8


def copy_for_each(value, axis):
    devices = lax.axis_size(axis)
    return lax.all_to_all(
        jnp.broadcast_to(value[None], (devices, *value.shape)), axis, 0, 0, tiled=True
    )


def taken_together(value, axis):
    return copy_for_each(value, axis).max(axis=0)


def packed_total(arrays, axis):
    ends = [0]
    for a in arrays:
        ends.append(ends[-1] + a.size)
    so_far = taken_together(jnp.concatenate([a.ravel() for a in arrays]), axis)
    return tuple((so_far[b:e].reshape(a.shape) for a, b, e in zip(arrays, ends, ends[1:])))


def in_one_piece(arrays, axis, dim, along):
    ends, at = ([], 0)
    for a in arrays[:-1]:
        at += a.shape[along]
        ends.append(at)
    both = jnp.concatenate(arrays, axis=along)
    return tuple(jnp.split(lax.all_gather(both, axis, axis=dim, tiled=True), ends, axis=along))


def local(w_gate, first_gate, second_gate, w_up, first_up, second_up, norm_train, norm_step):
    hold_gate = hold_rate * first_gate + second_gate
    latest_gate = w_gate - learn_rate * hold_gate
    hold_up = hold_rate * first_up + second_up
    latest_up = w_up - learn_rate * hold_up
    column_gate, column_up = packed_total(
        (jnp.max(jnp.abs(latest_gate), axis=0), jnp.max(jnp.abs(latest_up), axis=0)), "zero"
    )
    narrow_gate, narrow_up = (
        (latest_gate / column_gate).astype(jnp.bfloat16),
        (latest_up / column_up).astype(jnp.bfloat16),
    )
    ready_gate, ready_up = in_one_piece((narrow_gate, narrow_up), "zero", 0, 1)
    serve_norm = lax.all_gather(
        (norm_train + norm_step).astype(jnp.bfloat16), ("zero", "model"), axis=0, tiled=True
    )
    return (ready_gate, ready_up, column_gate, column_up, serve_norm, latest_gate, latest_up)


def solution(mesh):
    return jax.shard_map(
        local,
        mesh=mesh,
        in_specs=(
            P("zero", "model"),
            P("zero", "model"),
            P("zero", "model"),
            P("zero", "model"),
            P("zero", "model"),
            P("zero", "model"),
            P(("zero", "model")),
            P(("zero", "model")),
        ),
        out_specs=(
            P(None, "model"),
            P(None, "model"),
            P("model"),
            P("model"),
            P(),
            P("zero", "model"),
            P("zero", "model"),
        ),
        check_vma=False,
    )
```

profile of v0, /device:TPU:225, one launch (start us, length us, event | category | flops | bytes accessed | tf_op | source)
XLA Modules:
  0.0 147.3 jit_solution(10498429666778906284)
XLA Ops:
  7.2 0.0 all-gather.2.cloned.1.call-start
  7.2 3.4 %abs_reduce_fusion = (f32[432]{0:T(512)S(1)}, f32[640,432]{0,1:T(8,128)S(1)}, f32[432]{0:T(512)S(1)}, f32[640,432]{0,1:T(8,128)S(1)}) fusion(f32[640,432]{0,1:T(8,128)} %param.11, f32[640,432]{0,1:T(8,128)} %param.13, f32[640,432]{0,1:T(8,128)} %param.12, f32[640,432]{0,1:T(8,128)} %param.8, f32[640,432]{0,1:T(8,128)} %param.10, f32[640,432]{0,1:T(8,128)} %param.9), kind=kLoop, calls=%fused_computation.3 | loop fusion | flops 3316896 | bytes 8850816 | tf_op jit(solution)/shard_map/reduce_max | solution.py:44
  10.7 0.0 copy-start
  10.7 0.0 copy-start.1
  10.7 0.1 pad_maximum_fusion.1
  10.8 10.6 %all_to_all.6 = f32[8,1,864]{2,1,0:T(1,128)S(1)} all-to-all(f32[8,1,864]{2,1,0:T(1,128)S(1)} %broadcast_in_dim.2), channel_id=1, replica_groups=mesh['zero'=8,'model'=32] {'zero'}, dimensions={0} | all-to-all | bytes 55296 | tf_op jit(solution)/shard_map/all_to_all | solution.py:12
  21.4 0.1 fusion.1
  21.5 0.0 copy-start.2
  21.5 0.0 copy-start.3
  21.5 0.1 divide_convert_fusion.1
  21.6 0.1 divide_convert_fusion
  21.8 0.0 copy-done
  21.8 0.0 copy-done.1
  21.8 0.3 copy-done.2
  22.1 0.0 copy-done.3
  22.1 1.1 pad_maximum_fusion
  23.2 0.0 copy-start.4
  23.2 0.0 copy-start.5
  23.2 0.0 all-gather.2.cloned.1.call-update
  23.2 0.6 copy-done.4
  23.8 0.0 copy-done.5
  23.8 0.2 dynamic-update-slice
  24.1 108.7 %all-reduce = bf16[5120]{0:T(1024)(128)(2,1)} all-reduce(bf16[5120]{0:T(1024)(128)(2,1)S(1)} %dynamic-update-slice), channel_id=1, replica_groups=mesh['zero'=8,'model'=32] {'zero','model'}, use_global_device_ids=true, to_apply=%add | all-reduce | flops 5120 | bytes 20480
  132.7 0.0 all-gather.2.cloned.1.call-done
  132.7 7.7 %fusion = (bf16[5120,432]{0,1:T(8,128)(2,1)}, bf16[5120,432]{0,1:T(8,128)(2,1)}) fusion(bf16[5120,864]{0,1:T(8,128)(2,1)} %all-gather.2.cloned.1.call-done), kind=kLoop, calls=%fused_computation.9 | loop fusion | bytes 17694720 | tf_op jit(solution)/shard_map/split | solution.py:35
  (4 shorter events, 0.1 us)
Async XLA Ops:
  7.2 125.6 %all-gather.2.cloned.1.call-start = ((), (), s32[]{:S(2)}) async-start(), calls=%async_computation.1 | async-start | bytes 9953280 | tf_op jit(solution)/shard_map/all_gather | solution.py:35
  10.7 11.1 %copy-start = (f32[640,432]{0,1:T(8,128)}, f32[640,432]{0,1:T(8,128)S(1)}, u32[]{:S(2)}) copy-start(f32[640,432]{0,1:T(8,128)S(1)} %get-tuple-element.10) | copy-start | bytes 3317764
  10.7 11.1 %copy-start.1 = (f32[640,432]{0,1:T(8,128)}, f32[640,432]{0,1:T(8,128)S(1)}, u32[]{:S(2)}) copy-start(f32[640,432]{0,1:T(8,128)S(1)} %get-tuple-element.16) | copy-start | bytes 3317764
  21.5 0.6 copy-start.2
  21.5 0.6 copy-start.3
  23.2 0.7 copy-start.4
  23.2 0.7 copy-start.5
Sparse Core Ops, SparseCore 0:
  23.3 90.1 all-gather.1
where the time goes:
time: 148 us; the launch traced here: 147 us
  blocking collectives  119 us (80%)
  between operations  14.1 us (10%)
  local copies, waits for them, and re-layouts  8.99 us (6%)
  other arithmetic  4.91 us (3%)
    unnamed x1, blocking collectives  109 us
    all_to_all x1, blocking collectives, copy_for_each(): lax.all_to_all(jnp.broadcast_to(value[None], (devices, *value.shape)), ax...  10.6 us
    split x1, local copies, waits for them, and re-layouts, in_one_piece(): jnp.split(lax.all_gather(both, axis, axis=dim, tiled=True), ends, axis=al...  7.74 us
    reduce_max x1, other arithmetic, local(): jnp.max(jnp.abs(latest_up), axis=0)  3.44 us
  transfers between devices with their start and end apart: 1, of which 0 were waited for; matrix products, arithmetic and copies ran while one was open for 0% of the time, Pallas kernels for 0%

commit v1 on v0

v1 whole, which is shorter than its diff:
```python
import functools

import jax
import jax.numpy as jnp
from jax import lax
from jax.experimental import pallas as pl
from jax.experimental.pallas import tpu as pltpu
from jax.sharding import PartitionSpec as P

learn_rate = 0.25
hold_rate = 0.8

LANES = 128
CHUNK = 48
AHEAD = 4
ZERO, MODEL, PLANE = 8, 32, 16

f32, bf16 = jnp.float32, jnp.bfloat16


def iota(shape, dim):
    return lax.broadcasted_iota(jnp.int32, shape, dim)


def kernel(
    wg, fg, sg, wu, fu, su, nt, ns,
    rg, ru, lg, lu, cols, norm,
    stage, nin, mx, n1, nz, n3, wide,
    in_sem, nin_sem, mx_send, mx_recv, n_send, n1_recv, nz_recv, n3_recv,
    send_sem, own_recv, fwd_recv, d2d_send, d2d_recv,
):
    zero, model = lax.axis_index("zero"), lax.axis_index("model")
    rows_n, wide_n = lg.shape
    pieces = rows_n // CHUNK
    gathered, latest = (rg, ru), (lg, lu)
    high = lax.div(zero, 2)

    def at_zero(z):
        return {"zero": lax.rem(z, ZERO), "model": model}

    right, left = lax.rem(zero + 2, ZERO), lax.rem(zero + 6, ZERO)
    far = lax.rem(zero + 4, ZERO)
    mate = zero + 1 - 2 * lax.rem(zero, 2)
    plane0 = lax.div(model, PLANE) * PLANE
    spot = model - plane0
    other_plane = lax.rem(model + PLANE, MODEL)

    barrier = pltpu.get_barrier_semaphore()
    for j in range(1, ZERO):
        pl.semaphore_signal(barrier, inc=1, device_id=at_zero(zero + j))
    for j in range(1, PLANE):
        pl.semaphore_signal(
            barrier, inc=1, device_id={"zero": zero, "model": plane0 + lax.rem(spot + j, PLANE)}
        )

    @pl.when(high >= 2)
    def _():
        pl.semaphore_signal(barrier, inc=1, device_id={"zero": zero, "model": other_plane})

    loads = {}
    for k in range(pieces):
        for a, group in enumerate(((wg, fg, sg), (wu, fu, su))):
            for i, ref in enumerate(group):
                rows = pl.ds(k * CHUNK, CHUNK)
                loads[a, k, i] = pltpu.make_async_copy(
                    ref.at[rows], stage.at[a * 3 + i, rows], in_sem.at[a * 3 + i, k]
                )
                loads[a, k, i].start()
    norm_loads = [
        pltpu.make_async_copy(ref, nin.at[pl.ds(i, 1)], nin_sem.at[i])
        for i, ref in enumerate((nt, ns))
    ]
    for c in norm_loads:
        c.start()

    best = [None] * 8
    for k in range(pieces):
        rows = slice(k * CHUNK, (k + 1) * CHUNK)
        for a in range(2):
            for i in range(3):
                loads[a, k, i].wait()
            w, first, second = (stage[a * 3 + i, rows, :] for i in range(3))
            hold = hold_rate * first + second
            new = w - learn_rate * hold
            latest[a][rows, :] = new
            top = jnp.max(jnp.abs(new), axis=1, keepdims=True)
            at = iota((CHUNK, LANES), 0) + k * CHUNK - iota((CHUNK, LANES), 1)
            for r in range(k * CHUNK // LANES, ((k + 1) * CHUNK - 1) // LANES + 1):
                line = jnp.max(jnp.where(at == r * LANES, top, 0.0), axis=0, keepdims=True)
                old = best[a * 4 + r]
                best[a * 4 + r] = line if old is None else jnp.maximum(old, line)
    for r in range(8):
        mx[zero, pl.ds(r, 1), :] = best[r]

    for c in norm_loads:
        c.wait()
    part = jnp.concatenate(
        [nin[0:1, :] + nin[1:2, :], jnp.zeros((1, LANES - nin.shape[1]), f32)], axis=1
    ).astype(bf16).astype(f32)
    width = nin.shape[1]
    begin = model * width
    lane0 = lax.rem(begin, LANES)
    turned = pltpu.roll(jnp.broadcast_to(part, (8, LANES)), lane0, 1)
    place = iota((8, LANES), 0) * LANES + iota((8, LANES), 1) - begin
    n1[spot] = jnp.where((place >= 0) & (place < width), turned, 0.0)

    @pl.when(high < 2)
    def _():
        pl.semaphore_wait(barrier, ZERO - 1 + PLANE - 1)

    @pl.when(high >= 2)
    def _():
        pl.semaphore_wait(barrier, ZERO - 1 + PLANE)

    def remote(src, dst, send, recv, to):
        return pltpu.make_async_remote_copy(
            src_ref=src, dst_ref=dst, send_sem=send, recv_sem=recv, device_id=to,
            device_id_type=pl.DeviceIdType.MESH,
        )

    def bytes_of(ref, sem):
        pltpu.make_async_copy(ref, ref, sem).wait()

    for j in (4, 5, 3, 6, 2, 7, 1):
        remote(mx.at[zero], mx.at[zero], mx_send, mx_recv, at_zero(zero + j)).start()
    for j in range(1, PLANE):
        to = {"zero": zero, "model": plane0 + lax.rem(spot + j, PLANE)}
        remote(n1.at[spot], n1.at[spot], n_send, n1_recv, to).start()

    bytes_of(mx.at[pl.ds(0, ZERO - 1)], mx_recv)
    bytes_of(mx.at[pl.ds(0, ZERO - 1)], mx_send)
    most = jnp.max(mx[...], axis=0)
    cols[...] = most

    def part_of(a, k, z):
        return gathered[a].at[pl.ds(k * CHUNK, CHUNK), pl.ds(pl.multiple_of(z * wide_n, LANES), wide_n)]

    def normalise(k):
        rows = slice(k * CHUNK, (k + 1) * CHUNK)
        at = iota((CHUNK, LANES), 0) + k * CHUNK - iota((CHUNK, LANES), 1)
        for a in range(2):
            top = None
            for r in range(k * CHUNK // LANES, ((k + 1) * CHUNK - 1) // LANES + 1):
                line = jnp.broadcast_to(most[a * 4 + r : a * 4 + r + 1], (CHUNK, LANES))
                part = jnp.max(jnp.where(at == r * LANES, line, 0.0), axis=1, keepdims=True)
                top = part if top is None else jnp.maximum(top, part)
            scaled = latest[a][rows, :] * (1.0 / top)
            gathered[a][rows, pl.ds(pl.multiple_of(zero * wide_n, LANES), wide_n)] = scaled.astype(bf16)

    def push(a, k, z):
        ref = part_of(a, k, z)
        remote(ref, ref, d2d_send, d2d_recv.at[a], at_zero(mate)).start()

    steps = [(0, k) for k in range(pieces)] + [(1, k) for k in range(pieces)]

    def send_own(i):
        a, k = steps[i]
        if i < pieces:
            normalise(k)
        for way, (b, to) in enumerate(((a, right), (1 - a, left))):
            ref = part_of(b, k, zero)
            remote(ref, ref, send_sem.at[way], own_recv.at[way, i], at_zero(to)).start()
        if i < pieces:
            push(0, k, zero)
            push(1, k, zero)

    def arrive(way, i):
        a, k = steps[i]
        b, origin = ((a, left), (1 - a, right))[way]
        ref = part_of(b, k, origin)
        remote(ref, ref, send_sem.at[way], own_recv.at[way, i], at_zero(origin)).wait_recv()
        if i < pieces:
            to = (right, left)[way]
            remote(ref, ref, send_sem.at[way], fwd_recv.at[way, k], at_zero(to)).start()
        push(b, k, origin)

    def arrive_far(way, k):
        ref = part_of(way, k, far)
        remote(ref, ref, send_sem.at[way], fwd_recv.at[way, k], at_zero(far)).wait_recv()
        push(way, k, far)

    for i in range(AHEAD):
        send_own(i)
    far_done = 0
    for i in range(2 * pieces):
        for way in range(2):
            arrive(way, i)
        if i + AHEAD < 2 * pieces:
            send_own(i + AHEAD)
        if i > AHEAD and far_done < pieces:
            for way in range(2):
                arrive_far(way, far_done)
            far_done += 1
        if i == 0:
            bytes_of(n1.at[pl.ds(0, PLANE - 1)], n1_recv)
            bytes_of(n1.at[pl.ds(0, PLANE - 1)], n_send)
            nz[zero] = jnp.sum(n1[...], axis=0)
            for j in (4, 5, 3, 6, 2, 7, 1):
                remote(nz.at[zero], nz.at[zero], n_send, nz_recv, at_zero(zero + j)).start()
        if i == 5:
            bytes_of(nz.at[pl.ds(0, ZERO - 1)], nz_recv)
            bytes_of(nz.at[pl.ds(0, ZERO - 1)], n_send)

            @pl.when(high >= 2)
            def _():
                to = {"zero": zero, "model": other_plane}
                remote(nz, n3, n_send, n3_recv, to).start()

        if i == 10:

            @pl.when(high >= 2)
            def _():
                bytes_of(n3, n3_recv)
                bytes_of(n3, n_send)
                to = lax.rem(zero + 2 * (2 * high - 5) + ZERO, ZERO)
                remote(n3, n3, n_send, n3_recv, at_zero(to)).start()

    @pl.when(high >= 2)
    def _():
        bytes_of(n3, n_send)

    @pl.when(high < 2)
    def _():
        bytes_of(n3, n3_recv)

    for z in range(ZERO):
        wide[z * 5 : z * 5 + 5, :] = (nz[z] + n3[z])[0:5]
    norm[...] = wide[...].astype(bf16)

    for way in range(2):
        bytes_of(rg.at[:, pl.ds(0, 3 * wide_n)], send_sem.at[way])
    bytes_of(rg, d2d_send)
    for a in range(2):
        bytes_of(rg.at[:, pl.ds(0, 4 * wide_n)], d2d_recv.at[a])


def local(w_gate, first_gate, second_gate, w_up, first_up, second_up, norm_train, norm_step):
    weights = [v.T for v in (w_gate, first_gate, second_gate, w_up, first_up, second_up)]
    n, d = weights[0].shape
    small = norm_train.shape[0]
    pieces = n // CHUNK
    vmem, hbm = pl.BlockSpec(memory_space=pltpu.VMEM), pl.BlockSpec(memory_space=pltpu.HBM)
    dma = pltpu.SemaphoreType.DMA
    rg, ru, lg, lu, cols, norm = pl.pallas_call(
        kernel,
        out_shape=(
            pltpu.VMEM((n, ZERO * d), bf16),
            pltpu.VMEM((n, ZERO * d), bf16),
            pltpu.VMEM((n, d), f32),
            pltpu.VMEM((n, d), f32),
            pltpu.VMEM((8, LANES), f32),
            pltpu.VMEM((ZERO * MODEL * small // LANES, LANES), bf16),
        ),
        in_specs=[hbm] * 8,
        out_specs=(vmem,) * 6,
        scratch_shapes=[
            pltpu.VMEM((6, n, d), f32),
            pltpu.VMEM((2, small), f32),
            pltpu.VMEM((ZERO, 8, LANES), f32),
            pltpu.VMEM((PLANE, 8, LANES), f32),
            pltpu.VMEM((ZERO, 8, LANES), f32),
            pltpu.VMEM((ZERO, 8, LANES), f32),
            pltpu.VMEM((ZERO * MODEL * small // LANES, LANES), f32),
            dma((6, pieces)),
            dma((2,)),
            dma(()),
            dma(()),
            dma(()),
            dma(()),
            dma(()),
            dma(()),
            dma((2,)),
            dma((2, 2 * pieces)),
            dma((2, pieces)),
            dma(()),
            dma((2,)),
        ],
        compiler_params=pltpu.CompilerParams(
            collective_id=0, has_side_effects=True, vmem_limit_bytes=48 * 1024 * 1024
        ),
        name="update_gather",
    )(*weights, norm_train.reshape(1, small), norm_step.reshape(1, small))
    flat = cols.reshape(2, 4 * LANES)
    return rg.T, ru.T, flat[0, :n], flat[1, :n], norm.reshape(-1), lg.T, lu.T


def solution(mesh):
    return jax.shard_map(
        local,
        mesh=mesh,
        in_specs=(P("zero", "model"),) * 6 + (P(("zero", "model")),) * 2,
        out_specs=(
            P(None, "model"),
            P(None, "model"),
            P("model"),
            P("model"),
            P(),
            P("zero", "model"),
            P("zero", "model"),
        ),
        check_vma=False,
    )
```

time: 148 us -> 102 us (0.69)
  the two profiles are of different devices: /device:TPU:225 before, /device:TPU:1 now
where the time goes in v1:
time: 102 us
  Pallas kernels  93.7 us (92%)
  local copies, waits for them, and re-layouts  7.35 us (7%)
    pallas_call x1, Pallas kernels, local(): pl.pallas_call(kernel, out_shape=(pltpu.VMEM((n, ZERO * d), bf16), pltpu....  93.7 us
    unnamed x5, local copies, waits for them, and re-layouts  6.76 us

profile of v1, /device:TPU:1, one launch (start us, length us, event | category | flops | bytes accessed | tf_op | source)
XLA Modules:
  0.0 101.7 jit_solution(9310534208976482437)
XLA Ops:
  0.6 93.7 %update_gather.1 = (bf16[432,5120]{1,0:T(8,128)(2,1)S(1)}, bf16[432,5120]{1,0:T(8,128)(2,1)S(1)}, f32[432,640]{1,0:T(8,128)S(1)}, f32[432,640]{1,0:T(8,128)S(1)}...) custom-call(f32[432,640]{1,0:T(8,128)} %bitcast.20, f32[432,640]{1,0:T(8,128)} %bitcast.21, f32[432,640]{1,0:T(8,128)} %bitcast.22, ...), custom_call_target="tpu_custom_call" | custom-call | tf_op jit(solution)/shard_map/update_gather/pallas_call | solution.py:244
  94.3 2.1 %copy.20 = bf16[5120,432]{0,1:T(8,128)(2,1)} copy(bf16[5120,432]{0,1:T(8,128)(2,1)S(1)} %bitcast.16) | data formatting | bytes 8847360
  96.4 2.1 %copy.21 = bf16[5120,432]{0,1:T(8,128)(2,1)} copy(bf16[5120,432]{0,1:T(8,128)(2,1)S(1)} %bitcast.15) | data formatting | bytes 8847360
  98.5 0.6 fusion
  99.1 0.6 copy.22
  99.7 1.0 copy.23
  100.7 1.0 copy.24
  (1 shorter events, 0.0 us)

commit v2 on v1

--- a/solution.py
+++ b/solution.py
@@ -13,6 +13,7 @@
 LANES = 128
 CHUNK = 48
 AHEAD = 4
+WRITES = 4
 ZERO, MODEL, PLANE = 8, 32, 16
 
 f32, bf16 = jnp.float32, jnp.bfloat16
@@ -24,8 +25,8 @@
 
 def kernel(
     wg, fg, sg, wu, fu, su, nt, ns,
-    rg, ru, lg, lu, cols, norm,
-    stage, nin, mx, n1, nz, n3, wide,
+    rg, ru, lg, lu, cg, cu, norm,
+    stage, raw, nin, mx, n1, nz, n3, wide,
     in_sem, nin_sem, mx_send, mx_recv, n_send, n1_recv, nz_recv, n3_recv,
     send_sem, own_recv, fwd_recv, d2d_send, d2d_recv,
 ):
@@ -123,6 +124,10 @@
 
     for j in (4, 5, 3, 6, 2, 7, 1):
         remote(mx.at[zero], mx.at[zero], mx_send, mx_recv, at_zero(zero + j)).start()
+    for way, to in enumerate((right, left)):
+        remote(
+            latest[way].at[pl.ds(0, CHUNK)], raw.at[way], send_sem.at[way], own_recv.at[way, 0], at_zero(to)
+        ).start()
     for j in range(1, PLANE):
         to = {"zero": zero, "model": plane0 + lax.rem(spot + j, PLANE)}
         remote(n1.at[spot], n1.at[spot], n_send, n1_recv, to).start()
@@ -130,22 +135,33 @@
     bytes_of(mx.at[pl.ds(0, ZERO - 1)], mx_recv)
     bytes_of(mx.at[pl.ds(0, ZERO - 1)], mx_send)
     most = jnp.max(mx[...], axis=0)
-    cols[...] = most
+    for r in range(4):
+        some = min(LANES, rows_n - r * LANES)
+        cg[:, r * LANES : r * LANES + some] = most[r : r + 1, :some]
+        cu[:, r * LANES : r * LANES + some] = most[4 + r : 5 + r, :some]
 
     def part_of(a, k, z):
         return gathered[a].at[pl.ds(k * CHUNK, CHUNK), pl.ds(pl.multiple_of(z * wide_n, LANES), wide_n)]
 
+    def rate_of(a, k):
+        at = iota((CHUNK, LANES), 0) + k * CHUNK - iota((CHUNK, LANES), 1)
+        top = None
+        for r in range(k * CHUNK // LANES, ((k + 1) * CHUNK - 1) // LANES + 1):
+            line = jnp.broadcast_to(most[a * 4 + r : a * 4 + r + 1], (CHUNK, LANES))
+            part = jnp.max(jnp.where(at == r * LANES, line, 0.0), axis=1, keepdims=True)
+            top = part if top is None else jnp.maximum(top, part)
+        return 1.0 / top
+
+    def keep(a, k, z, values, rate):
+        columns = pl.ds(pl.multiple_of(z * wide_n, LANES), wide_n)
+        gathered[a][k * CHUNK : (k + 1) * CHUNK, columns] = (values * rate).astype(bf16)
+
+    rates0 = [rate_of(a, 0) for a in range(2)]
+
     def normalise(k):
-        rows = slice(k * CHUNK, (k + 1) * CHUNK)
-        at = iota((CHUNK, LANES), 0) + k * CHUNK - iota((CHUNK, LANES), 1)
         for a in range(2):
-            top = None
-            for r in range(k * CHUNK // LANES, ((k + 1) * CHUNK - 1) // LANES + 1):
-                line = jnp.broadcast_to(most[a * 4 + r : a * 4 + r + 1], (CHUNK, LANES))
-                part = jnp.max(jnp.where(at == r * LANES, line, 0.0), axis=1, keepdims=True)
-                top = part if top is None else jnp.maximum(top, part)
-            scaled = latest[a][rows, :] * (1.0 / top)
-            gathered[a][rows, pl.ds(pl.multiple_of(zero * wide_n, LANES), wide_n)] = scaled.astype(bf16)
+            rate = rates0[a] if k == 0 else rate_of(a, k)
+            keep(a, k, zero, latest[a][k * CHUNK : (k + 1) * CHUNK, :], rate)
 
     def push(a, k, z):
         ref = part_of(a, k, z)
@@ -158,6 +174,8 @@
         if i < pieces:
             normalise(k)
         for way, (b, to) in enumerate(((a, right), (1 - a, left))):
+            if i == 0:
+                continue
             ref = part_of(b, k, zero)
             remote(ref, ref, send_sem.at[way], own_recv.at[way, i], at_zero(to)).start()
         if i < pieces:
@@ -168,7 +186,11 @@
         a, k = steps[i]
         b, origin = ((a, left), (1 - a, right))[way]
         ref = part_of(b, k, origin)
-        remote(ref, ref, send_sem.at[way], own_recv.at[way, i], at_zero(origin)).wait_recv()
+        if i == 0:
+            bytes_of(raw.at[way], own_recv.at[way, 0])
+            keep(b, k, origin, raw[way], rates0[b])
+        else:
+            remote(ref, ref, send_sem.at[way], own_recv.at[way, i], at_zero(origin)).wait_recv()
         if i < pieces:
             to = (right, left)[way]
             remote(ref, ref, send_sem.at[way], fwd_recv.at[way, k], at_zero(to)).start()
@@ -228,10 +250,32 @@
     norm[...] = wide[...].astype(bf16)
 
     for way in range(2):
-        bytes_of(rg.at[:, pl.ds(0, 3 * wide_n)], send_sem.at[way])
+        bytes_of(rg.at[pl.ds(0, (rows_n * 3 + CHUNK) // 4), pl.ds(0, 4 * wide_n)], send_sem.at[way])
     bytes_of(rg, d2d_send)
     for a in range(2):
         bytes_of(rg.at[:, pl.ds(0, 4 * wide_n)], d2d_recv.at[a])
+
+
+def writer(rg, ru, lg, lu, cg, cu, norm, rg_o, ru_o, cg_o, cu_o, norm_o, lg_o, lu_o, sems):
+    copies = []
+
+    def out(src, dst):
+        copies.append(pltpu.make_async_copy(src, dst, sems.at[len(copies)]))
+        copies[-1].start()
+
+    n = rg.shape[0]
+    step = -(-n // WRITES // 8) * 8
+    for src, dst in ((rg, rg_o), (ru, ru_o)):
+        for at in range(0, n, step):
+            rows = pl.ds(at, min(step, n - at))
+            out(src.at[rows], dst.at[rows])
+    out(lg, lg_o)
+    out(lu, lu_o)
+    out(cg, cg_o)
+    out(cu, cu_o)
+    out(norm, norm_o)
+    for c in copies:
+        c.wait()
 
 
 def local(w_gate, first_gate, second_gate, w_up, first_up, second_up, norm_train, norm_step):
@@ -239,28 +283,31 @@
     n, d = weights[0].shape
     small = norm_train.shape[0]
     pieces = n // CHUNK
+    lines = ZERO * MODEL * small // LANES
     vmem, hbm = pl.BlockSpec(memory_space=pltpu.VMEM), pl.BlockSpec(memory_space=pltpu.HBM)
     dma = pltpu.SemaphoreType.DMA
-    rg, ru, lg, lu, cols, norm = pl.pallas_call(
+    held = pl.pallas_call(
         kernel,
         out_shape=(
             pltpu.VMEM((n, ZERO * d), bf16),
             pltpu.VMEM((n, ZERO * d), bf16),
             pltpu.VMEM((n, d), f32),
             pltpu.VMEM((n, d), f32),
-            pltpu.VMEM((8, LANES), f32),
-            pltpu.VMEM((ZERO * MODEL * small // LANES, LANES), bf16),
+            pltpu.VMEM((1, n), f32),
+            pltpu.VMEM((1, n), f32),
+            pltpu.VMEM((lines, LANES), bf16),
         ),
         in_specs=[hbm] * 8,
-        out_specs=(vmem,) * 6,
+        out_specs=(vmem,) * 7,
         scratch_shapes=[
             pltpu.VMEM((6, n, d), f32),
+            pltpu.VMEM((2, CHUNK, d), f32),
             pltpu.VMEM((2, small), f32),
             pltpu.VMEM((ZERO, 8, LANES), f32),
             pltpu.VMEM((PLANE, 8, LANES), f32),
             pltpu.VMEM((ZERO, 8, LANES), f32),
             pltpu.VMEM((ZERO, 8, LANES), f32),
-            pltpu.VMEM((ZERO * MODEL * small // LANES, LANES), f32),
+            pltpu.VMEM((lines, LANES), f32),
             dma((6, pieces)),
             dma((2,)),
             dma(()),
@@ -280,8 +327,24 @@
         ),
         name="update_gather",
     )(*weights, norm_train.reshape(1, small), norm_step.reshape(1, small))
-    flat = cols.reshape(2, 4 * LANES)
-    return rg.T, ru.T, flat[0, :n], flat[1, :n], norm.reshape(-1), lg.T, lu.T
+    rg, ru, cg, cu, norm, lg, lu = pl.pallas_call(
+        writer,
+        out_shape=(
+            pltpu.HBM((n, ZERO * d), bf16),
+            pltpu.HBM((n, ZERO * d), bf16),
+            pltpu.HBM((1, n), f32),
+            pltpu.HBM((1, n), f32),
+            pltpu.HBM((lines, LANES), bf16),
+            pltpu.HBM((n, d), f32),
+            pltpu.HBM((n, d), f32),
+        ),
+        in_specs=[vmem] * 7,
+        out_specs=(hbm,) * 7,
+        scratch_shapes=[dma((2 * WRITES + 5,))],
+        compiler_params=pltpu.CompilerParams(vmem_limit_bytes=48 * 1024 * 1024),
+        name="write_out",
+    )(*[pltpu.with_memory_space_constraint(v, pltpu.VMEM) for v in held])
+    return rg.T, ru.T, cg.reshape(-1), cu.reshape(-1), norm.reshape(-1), lg.T, lu.T
 
 
 def solution(mesh):

time: 102 us -> 98 us (0.961)
  local copies, waits for them, and re-layouts: 7.35 us -> 0 us
  Pallas kernels: 93.7 us -> 97.2 us
    unnamed x5 -> x0, local copies, waits for them, and re-layouts: 6.76 us -> none
    pallas_call x0 -> x1, Pallas kernels: none -> 4.23 us  [local(): pl.pallas_call(writer, out_shape=(pltpu.HBM((n, ZERO * d), bf16), pltpu.H...]
where the time goes in v2:
time: 98 us; the launch traced here: 97.9 us
  Pallas kernels  97.2 us (99%)
    pallas_call x1, Pallas kernels, local(): pl.pallas_call(kernel, out_shape=(pltpu.VMEM((n, ZERO * d), bf16), pltpu....  93 us
    pallas_call x1, Pallas kernels, local(): pl.pallas_call(writer, out_shape=(pltpu.HBM((n, ZERO * d), bf16), pltpu.H...  4.23 us

profile of v2, /device:TPU:1, one launch (start us, length us, event | category | flops | bytes accessed | tf_op | source)
XLA Modules:
  0.0 97.9 jit_solution(15101273769241148617)
XLA Ops:
  0.6 93.0 %update_gather.1 = (bf16[432,5120]{1,0:T(8,128)(2,1)S(1)}, bf16[432,5120]{1,0:T(8,128)(2,1)S(1)}, f32[432,640]{1,0:T(8,128)S(1)}, f32[432,640]{1,0:T(8,128)S(1)}...) custom-call(f32[432,640]{1,0:T(8,128)} %bitcast.15, f32[432,640]{1,0:T(8,128)} %bitcast.16, ...), custom_call_target="tpu_custom_call" | custom-call | tf_op jit(solution)/shard_map/update_gather/pallas_call | solution.py:289
  93.6 4.2 %write_out.1 = (bf16[432,5120]{1,0:T(8,128)(2,1)}, bf16[432,5120]{1,0:T(8,128)(2,1)}, f32[1,432]{1,0:T(1,128)}, f32[1,432]{1,0:T(1,128)}, bf16[40,128]{1,0:T(8,1...) custom-call(bf16[432,5120]{1,0:T(8,128)(2,1)S(1)} %get-tuple-element.21.rg, ...), custom_call_target="tpu_custom_call" | custom-call | tf_op jit(solution)/shard_map/write_out/pallas_call | solution.py:330

commit v3 on v2

--- a/solution.py
+++ b/solution.py
@@ -13,8 +13,10 @@
 LANES = 128
 CHUNK = 48
 AHEAD = 4
+EARLY = 1
+LOADS = 3
 WRITES = 4
-ZERO, MODEL, PLANE = 8, 32, 16
+ZERO, MODEL, SIDE = 8, 32, 4
 
 f32, bf16 = jnp.float32, jnp.bfloat16
 
@@ -26,8 +28,8 @@
 def kernel(
     wg, fg, sg, wu, fu, su, nt, ns,
     rg, ru, lg, lu, cg, cu, norm,
-    stage, raw, nin, mx, n1, nz, n3, wide,
-    in_sem, nin_sem, mx_send, mx_recv, n_send, n1_recv, nz_recv, n3_recv,
+    stage, raw, peak, nin, mx, n1, n2, nz, n3, wide,
+    in_sem, nin_sem, mx_send, mx_recv, n_send, n1_recv, n2_recv, nz_recv, n3_recv,
     send_sem, own_recv, fwd_recv, d2d_send, d2d_recv,
 ):
     zero, model = lax.axis_index("zero"), lax.axis_index("model")
@@ -42,27 +44,32 @@
     right, left = lax.rem(zero + 2, ZERO), lax.rem(zero + 6, ZERO)
     far = lax.rem(zero + 4, ZERO)
     mate = zero + 1 - 2 * lax.rem(zero, 2)
-    plane0 = lax.div(model, PLANE) * PLANE
-    spot = model - plane0
-    other_plane = lax.rem(model + PLANE, MODEL)
+    x, y = lax.rem(model, SIDE), lax.rem(lax.div(model, SIDE), SIDE)
+    other_plane = lax.rem(model + MODEL // 2, MODEL)
+
+    def at_x(j):
+        return {"zero": zero, "model": model - x + lax.rem(x + j, SIDE)}
+
+    def at_y(j):
+        return {"zero": zero, "model": model + (lax.rem(y + j, SIDE) - y) * SIDE}
 
     barrier = pltpu.get_barrier_semaphore()
     for j in range(1, ZERO):
         pl.semaphore_signal(barrier, inc=1, device_id=at_zero(zero + j))
-    for j in range(1, PLANE):
-        pl.semaphore_signal(
-            barrier, inc=1, device_id={"zero": zero, "model": plane0 + lax.rem(spot + j, PLANE)}
-        )
+    for j in range(1, SIDE):
+        pl.semaphore_signal(barrier, inc=1, device_id=at_x(j))
+        pl.semaphore_signal(barrier, inc=1, device_id=at_y(j))
 
     @pl.when(high >= 2)
     def _():
         pl.semaphore_signal(barrier, inc=1, device_id={"zero": zero, "model": other_plane})
 
     loads = {}
-    for k in range(pieces):
+    some = rows_n // LOADS
+    for k in range(LOADS):
         for a, group in enumerate(((wg, fg, sg), (wu, fu, su))):
             for i, ref in enumerate(group):
-                rows = pl.ds(k * CHUNK, CHUNK)
+                rows = pl.ds(k * some, some)
                 loads[a, k, i] = pltpu.make_async_copy(
                     ref.at[rows], stage.at[a * 3 + i, rows], in_sem.at[a * 3 + i, k]
                 )
@@ -74,17 +81,25 @@
     for c in norm_loads:
         c.start()
 
-    best = [None] * 8
     for k in range(pieces):
         rows = slice(k * CHUNK, (k + 1) * CHUNK)
         for a in range(2):
-            for i in range(3):
-                loads[a, k, i].wait()
+            if k * CHUNK % some == 0:
+                for i in range(3):
+                    loads[a, k * CHUNK // some, i].wait()
             w, first, second = (stage[a * 3 + i, rows, :] for i in range(3))
             hold = hold_rate * first + second
             new = w - learn_rate * hold
             latest[a][rows, :] = new
-            top = jnp.max(jnp.abs(new), axis=1, keepdims=True)
+            size = jnp.abs(new)
+            tall = size[:, :LANES]
+            for at in range(LANES, wide_n, LANES):
+                tall = jnp.maximum(tall, size[:, at : at + LANES])
+            peak[a, rows, :] = tall
+    best = [None] * 8
+    for k in range(pieces):
+        for a in range(2):
+            top = jnp.max(peak[a, k * CHUNK : (k + 1) * CHUNK, :], axis=1, keepdims=True)
             at = iota((CHUNK, LANES), 0) + k * CHUNK - iota((CHUNK, LANES), 1)
             for r in range(k * CHUNK // LANES, ((k + 1) * CHUNK - 1) // LANES + 1):
                 line = jnp.max(jnp.where(at == r * LANES, top, 0.0), axis=0, keepdims=True)
@@ -103,15 +118,15 @@
     lane0 = lax.rem(begin, LANES)
     turned = pltpu.roll(jnp.broadcast_to(part, (8, LANES)), lane0, 1)
     place = iota((8, LANES), 0) * LANES + iota((8, LANES), 1) - begin
-    n1[spot] = jnp.where((place >= 0) & (place < width), turned, 0.0)
+    n1[x] = jnp.where((place >= 0) & (place < width), turned, 0.0)
 
     @pl.when(high < 2)
     def _():
-        pl.semaphore_wait(barrier, ZERO - 1 + PLANE - 1)
+        pl.semaphore_wait(barrier, ZERO - 1 + 2 * (SIDE - 1))
 
     @pl.when(high >= 2)
     def _():
-        pl.semaphore_wait(barrier, ZERO - 1 + PLANE)
+        pl.semaphore_wait(barrier, ZERO + 2 * (SIDE - 1))
 
     def remote(src, dst, send, recv, to):
         return pltpu.make_async_remote_copy(
@@ -124,13 +139,17 @@
 
     for j in (4, 5, 3, 6, 2, 7, 1):
         remote(mx.at[zero], mx.at[zero], mx_send, mx_recv, at_zero(zero + j)).start()
-    for way, to in enumerate((right, left)):
-        remote(
-            latest[way].at[pl.ds(0, CHUNK)], raw.at[way], send_sem.at[way], own_recv.at[way, 0], at_zero(to)
-        ).start()
-    for j in range(1, PLANE):
-        to = {"zero": zero, "model": plane0 + lax.rem(spot + j, PLANE)}
-        remote(n1.at[spot], n1.at[spot], n_send, n1_recv, to).start()
+    for i in range(EARLY):
+        for way, to in enumerate((right, left)):
+            remote(
+                latest[way].at[pl.ds(i * CHUNK, CHUNK)],
+                raw.at[way, i],
+                send_sem.at[way],
+                own_recv.at[way, i],
+                at_zero(to),
+            ).start()
+    for j in range(1, SIDE):
+        remote(n1.at[x], n1.at[x], n_send, n1_recv, at_x(j)).start()
 
     bytes_of(mx.at[pl.ds(0, ZERO - 1)], mx_recv)
     bytes_of(mx.at[pl.ds(0, ZERO - 1)], mx_send)
@@ -156,17 +175,18 @@
         columns = pl.ds(pl.multiple_of(z * wide_n, LANES), wide_n)
         gathered[a][k * CHUNK : (k + 1) * CHUNK, columns] = (values * rate).astype(bf16)
 
-    rates0 = [rate_of(a, 0) for a in range(2)]
+    rates = {}
 
     def normalise(k):
         for a in range(2):
-            rate = rates0[a] if k == 0 else rate_of(a, k)
-            keep(a, k, zero, latest[a][k * CHUNK : (k + 1) * CHUNK, :], rate)
+            rates[a, k] = rate_of(a, k)
+            keep(a, k, zero, latest[a][k * CHUNK : (k + 1) * CHUNK, :], rates[a, k])
 
     def push(a, k, z):
         ref = part_of(a, k, z)
         remote(ref, ref, d2d_send, d2d_recv.at[a], at_zero(mate)).start()
 
+    gain_at = [2 * pieces * v // 18 for v in (0, 2, 6, 11, 15)]
     steps = [(0, k) for k in range(pieces)] + [(1, k) for k in range(pieces)]
 
     def send_own(i):
@@ -174,7 +194,7 @@
         if i < pieces:
             normalise(k)
         for way, (b, to) in enumerate(((a, right), (1 - a, left))):
-            if i == 0:
+            if i < EARLY:
                 continue
             ref = part_of(b, k, zero)
             remote(ref, ref, send_sem.at[way], own_recv.at[way, i], at_zero(to)).start()
@@ -186,9 +206,9 @@
         a, k = steps[i]
         b, origin = ((a, left), (1 - a, right))[way]
         ref = part_of(b, k, origin)
-        if i == 0:
-            bytes_of(raw.at[way], own_recv.at[way, 0])
-            keep(b, k, origin, raw[way], rates0[b])
+        if i < EARLY:
+            bytes_of(raw.at[way, i], own_recv.at[way, i])
+            keep(b, k, origin, raw[way, i], rates[b, k])
         else:
             remote(ref, ref, send_sem.at[way], own_recv.at[way, i], at_zero(origin)).wait_recv()
         if i < pieces:
@@ -213,13 +233,19 @@
             for way in range(2):
                 arrive_far(way, far_done)
             far_done += 1
-        if i == 0:
-            bytes_of(n1.at[pl.ds(0, PLANE - 1)], n1_recv)
-            bytes_of(n1.at[pl.ds(0, PLANE - 1)], n_send)
-            nz[zero] = jnp.sum(n1[...], axis=0)
+        if i == gain_at[0]:
+            bytes_of(n1.at[pl.ds(0, SIDE - 1)], n1_recv)
+            bytes_of(n1.at[pl.ds(0, SIDE - 1)], n_send)
+            n2[y] = jnp.sum(n1[...], axis=0)
+            for j in range(1, SIDE):
+                remote(n2.at[y], n2.at[y], n_send, n2_recv, at_y(j)).start()
+        if i == gain_at[1]:
+            bytes_of(n2.at[pl.ds(0, SIDE - 1)], n2_recv)
+            bytes_of(n2.at[pl.ds(0, SIDE - 1)], n_send)
+            nz[zero] = jnp.sum(n2[...], axis=0)
             for j in (4, 5, 3, 6, 2, 7, 1):
                 remote(nz.at[zero], nz.at[zero], n_send, nz_recv, at_zero(zero + j)).start()
-        if i == 5:
+        if i == gain_at[2]:
             bytes_of(nz.at[pl.ds(0, ZERO - 1)], nz_recv)
             bytes_of(nz.at[pl.ds(0, ZERO - 1)], n_send)
 
@@ -228,7 +254,7 @@
                 to = {"zero": zero, "model": other_plane}
                 remote(nz, n3, n_send, n3_recv, to).start()
 
-        if i == 10:
+        if i == gain_at[3]:
 
             @pl.when(high >= 2)
             def _():
@@ -237,20 +263,23 @@
                 to = lax.rem(zero + 2 * (2 * high - 5) + ZERO, ZERO)
                 remote(n3, n3, n_send, n3_recv, at_zero(to)).start()
 
-    @pl.when(high >= 2)
-    def _():
-        bytes_of(n3, n_send)
-
-    @pl.when(high < 2)
-    def _():
-        bytes_of(n3, n3_recv)
-
-    for z in range(ZERO):
-        wide[z * 5 : z * 5 + 5, :] = (nz[z] + n3[z])[0:5]
-    norm[...] = wide[...].astype(bf16)
+        if i == gain_at[4]:
+            @pl.when(high >= 2)
+            def _():
+                bytes_of(n3, n_send)
+
+            @pl.when(high < 2)
+            def _():
+                bytes_of(n3, n3_recv)
+
+            for z in range(ZERO):
+                wide[z * 5 : z * 5 + 5, :] = (nz[z] + n3[z])[0:5]
+            norm[...] = wide[...].astype(bf16)
 
     for way in range(2):
-        bytes_of(rg.at[pl.ds(0, (rows_n * 3 + CHUNK) // 4), pl.ds(0, 4 * wide_n)], send_sem.at[way])
+        total = rows_n * 3 + EARLY * CHUNK
+        blocks = next(b for b in range(3, ZERO + 1) if total % (8 * b) == 0 and total // b <= rows_n)
+        bytes_of(rg.at[pl.ds(0, total // blocks), pl.ds(0, blocks * wide_n)], send_sem.at[way])
     bytes_of(rg, d2d_send)
     for a in range(2):
         bytes_of(rg.at[:, pl.ds(0, 4 * wide_n)], d2d_recv.at[a])
@@ -301,15 +330,18 @@
         out_specs=(vmem,) * 7,
         scratch_shapes=[
             pltpu.VMEM((6, n, d), f32),
-            pltpu.VMEM((2, CHUNK, d), f32),
+            pltpu.VMEM((2, max(EARLY, 1), CHUNK, d), f32),
+            pltpu.VMEM((2, n, LANES), f32),
             pltpu.VMEM((2, small), f32),
             pltpu.VMEM((ZERO, 8, LANES), f32),
-            pltpu.VMEM((PLANE, 8, LANES), f32),
+            pltpu.VMEM((SIDE, 8, LANES), f32),
+            pltpu.VMEM((SIDE, 8, LANES), f32),
             pltpu.VMEM((ZERO, 8, LANES), f32),
             pltpu.VMEM((ZERO, 8, LANES), f32),
             pltpu.VMEM((lines, LANES), f32),
-            dma((6, pieces)),
+            dma((6, LOADS)),
             dma((2,)),
+            dma(()),
             dma(()),
             dma(()),
             dma(()),

time: 98 us -> 95.1 us (0.970)
  Pallas kernels: 97.2 us -> 94.4 us
    pallas_call x1, Pallas kernels: 93 us -> 90.2 us  [local(): pl.pallas_call(kernel, out_shape=(pltpu.VMEM((n, ZERO * d), bf16), pltpu....]
where the time goes in v3:
time: 95.1 us; the launch traced here: 95 us
  Pallas kernels  94.4 us (99%)
    pallas_call x1, Pallas kernels, local(): pl.pallas_call(kernel, out_shape=(pltpu.VMEM((n, ZERO * d), bf16), pltpu....  90.2 us
    pallas_call x1, Pallas kernels, local(): pl.pallas_call(writer, out_shape=(pltpu.HBM((n, ZERO * d), bf16), pltpu.H...  4.23 us

profile of v3, /device:TPU:1, one launch (start us, length us, event | category | flops | bytes accessed | tf_op | source)
XLA Modules:
  0.0 95.0 jit_solution(4855288360183431370)
XLA Ops:
  0.6 90.2 %update_gather.1 = (bf16[432,5120]{1,0:T(8,128)(2,1)S(1)}, bf16[432,5120]{1,0:T(8,128)(2,1)S(1)}, f32[432,640]{1,0:T(8,128)S(1)}, f32[432,640]{1,0:T(8,128)S(1)}...) custom-call(f32[432,640]{1,0:T(8,128)} %bitcast.15, f32[432,640]{1,0:T(8,128)} %bitcast.16, ...), custom_call_target="tpu_custom_call" | custom-call | tf_op jit(solution)/shard_map/update_gather/pallas_call | solution.py:318
  90.8 4.2 %write_out.1 = (bf16[432,5120]{1,0:T(8,128)(2,1)}, bf16[432,5120]{1,0:T(8,128)(2,1)}, f32[1,432]{1,0:T(1,128)}, f32[1,432]{1,0:T(1,128)}, bf16[40,128]{1,0:T(8,1...) custom-call(bf16[432,5120]{1,0:T(8,128)(2,1)S(1)} %get-tuple-element.21.rg, ...), custom_call_target="tpu_custom_call" | custom-call | tf_op jit(solution)/shard_map/write_out/pallas_call | solution.py:362

commit v4 on v3

--- a/solution.py
+++ b/solution.py
@@ -12,7 +12,7 @@
 
 LANES = 128
 CHUNK = 48
-AHEAD = 4
+AHEAD = 6
 EARLY = 1
 LOADS = 3
 WRITES = 4
@@ -28,15 +28,14 @@
 def kernel(
     wg, fg, sg, wu, fu, su, nt, ns,
     rg, ru, lg, lu, cg, cu, norm,
-    stage, raw, peak, nin, mx, n1, n2, nz, n3, wide,
-    in_sem, nin_sem, mx_send, mx_recv, n_send, n1_recv, n2_recv, nz_recv, n3_recv,
-    send_sem, own_recv, fwd_recv, d2d_send, d2d_recv,
+    stage, raw, peak, nin, mx, n1, n2, n3, nz, wide,
+    in_sem, nin_sem, mx_send, mx_recv, n_send, n1_recv, n2_recv, n3_recv, nz_recv, nm_recv,
+    early_send, send_sem, own_recv, fwd_recv, d2d_send, d2d_recv,
 ):
     zero, model = lax.axis_index("zero"), lax.axis_index("model")
     rows_n, wide_n = lg.shape
     pieces = rows_n // CHUNK
     gathered, latest = (rg, ru), (lg, lu)
-    high = lax.div(zero, 2)
 
     def at_zero(z):
         return {"zero": lax.rem(z, ZERO), "model": model}
@@ -45,7 +44,7 @@
     far = lax.rem(zero + 4, ZERO)
     mate = zero + 1 - 2 * lax.rem(zero, 2)
     x, y = lax.rem(model, SIDE), lax.rem(lax.div(model, SIDE), SIDE)
-    other_plane = lax.rem(model + MODEL // 2, MODEL)
+    beside = {"zero": zero, "model": lax.rem(model + MODEL // 2, MODEL)}
 
     def at_x(j):
         return {"zero": zero, "model": model - x + lax.rem(x + j, SIDE)}
@@ -60,9 +59,7 @@
         pl.semaphore_signal(barrier, inc=1, device_id=at_x(j))
         pl.semaphore_signal(barrier, inc=1, device_id=at_y(j))
 
-    @pl.when(high >= 2)
-    def _():
-        pl.semaphore_signal(barrier, inc=1, device_id={"zero": zero, "model": other_plane})
+    pl.semaphore_signal(barrier, inc=1, device_id=beside)
 
     loads = {}
     some = rows_n // LOADS
@@ -118,15 +115,9 @@
     lane0 = lax.rem(begin, LANES)
     turned = pltpu.roll(jnp.broadcast_to(part, (8, LANES)), lane0, 1)
     place = iota((8, LANES), 0) * LANES + iota((8, LANES), 1) - begin
-    n1[x] = jnp.where((place >= 0) & (place < width), turned, 0.0)
-
-    @pl.when(high < 2)
-    def _():
-        pl.semaphore_wait(barrier, ZERO - 1 + 2 * (SIDE - 1))
-
-    @pl.when(high >= 2)
-    def _():
-        pl.semaphore_wait(barrier, ZERO + 2 * (SIDE - 1))
+    n1[x] = jnp.where((place >= 0) & (place < width), turned, 0.0).astype(bf16)
+
+    pl.semaphore_wait(barrier, ZERO + 2 * (SIDE - 1))
 
     def remote(src, dst, send, recv, to):
         return pltpu.make_async_remote_copy(
@@ -144,7 +135,7 @@
             remote(
                 latest[way].at[pl.ds(i * CHUNK, CHUNK)],
                 raw.at[way, i],
-                send_sem.at[way],
+                early_send,
                 own_recv.at[way, i],
                 at_zero(to),
             ).start()
@@ -186,7 +177,7 @@
         ref = part_of(a, k, z)
         remote(ref, ref, d2d_send, d2d_recv.at[a], at_zero(mate)).start()
 
-    gain_at = [2 * pieces * v // 18 for v in (0, 2, 6, 11, 15)]
+    gain_at = [2 * pieces * v // 18 for v in (0, 2, 5, 9, 14)]
     steps = [(0, k) for k in range(pieces)] + [(1, k) for k in range(pieces)]
 
     def send_own(i):
@@ -236,50 +227,38 @@
         if i == gain_at[0]:
             bytes_of(n1.at[pl.ds(0, SIDE - 1)], n1_recv)
             bytes_of(n1.at[pl.ds(0, SIDE - 1)], n_send)
-            n2[y] = jnp.sum(n1[...], axis=0)
+            n2[y] = jnp.sum(n1[...].astype(f32), axis=0).astype(bf16)
             for j in range(1, SIDE):
                 remote(n2.at[y], n2.at[y], n_send, n2_recv, at_y(j)).start()
         if i == gain_at[1]:
             bytes_of(n2.at[pl.ds(0, SIDE - 1)], n2_recv)
             bytes_of(n2.at[pl.ds(0, SIDE - 1)], n_send)
-            nz[zero] = jnp.sum(n2[...], axis=0)
-            for j in (4, 5, 3, 6, 2, 7, 1):
-                remote(nz.at[zero], nz.at[zero], n_send, nz_recv, at_zero(zero + j)).start()
+            n3[0] = jnp.sum(n2[...].astype(f32), axis=0).astype(bf16)
+            remote(n3.at[0], n3.at[1], n_send, n3_recv, beside).start()
         if i == gain_at[2]:
-            bytes_of(nz.at[pl.ds(0, ZERO - 1)], nz_recv)
-            bytes_of(nz.at[pl.ds(0, ZERO - 1)], n_send)
-
-            @pl.when(high >= 2)
-            def _():
-                to = {"zero": zero, "model": other_plane}
-                remote(nz, n3, n_send, n3_recv, to).start()
-
+            bytes_of(n3.at[1], n3_recv)
+            bytes_of(n3.at[0], n_send)
+            nz[zero] = jnp.sum(n3[...].astype(f32), axis=0).astype(bf16)
+            for z in (far, left, right):
+                remote(nz.at[zero], nz.at[zero], n_send, nz_recv, at_zero(z)).start()
         if i == gain_at[3]:
-
-            @pl.when(high >= 2)
-            def _():
-                bytes_of(n3, n3_recv)
-                bytes_of(n3, n_send)
-                to = lax.rem(zero + 2 * (2 * high - 5) + ZERO, ZERO)
-                remote(n3, n3, n_send, n3_recv, at_zero(to)).start()
-
+            bytes_of(nz.at[pl.ds(0, 3)], nz_recv)
+            bytes_of(nz.at[pl.ds(0, 3)], n_send)
+            for z in (zero, far, left, right):
+                remote(nz.at[z], nz.at[z], n_send, nm_recv, at_zero(mate)).start()
         if i == gain_at[4]:
-            @pl.when(high >= 2)
-            def _():
-                bytes_of(n3, n_send)
-
-            @pl.when(high < 2)
-            def _():
-                bytes_of(n3, n3_recv)
-
+            bytes_of(nz.at[pl.ds(0, 4)], nm_recv)
+            bytes_of(nz.at[pl.ds(0, 4)], n_send)
             for z in range(ZERO):
-                wide[z * 5 : z * 5 + 5, :] = (nz[z] + n3[z])[0:5]
+                wide[z * 5 : z * 5 + 5, :] = nz[z].astype(f32)[0:5]
             norm[...] = wide[...].astype(bf16)
 
     for way in range(2):
-        total = rows_n * 3 + EARLY * CHUNK
+        total = rows_n * 3 - EARLY * CHUNK
         blocks = next(b for b in range(3, ZERO + 1) if total % (8 * b) == 0 and total // b <= rows_n)
         bytes_of(rg.at[pl.ds(0, total // blocks), pl.ds(0, blocks * wide_n)], send_sem.at[way])
+    if EARLY:
+        bytes_of(raw, early_send)
     bytes_of(rg, d2d_send)
     for a in range(2):
         bytes_of(rg.at[:, pl.ds(0, 4 * wide_n)], d2d_recv.at[a])
@@ -334,13 +313,15 @@
             pltpu.VMEM((2, n, LANES), f32),
             pltpu.VMEM((2, small), f32),
             pltpu.VMEM((ZERO, 8, LANES), f32),
-            pltpu.VMEM((SIDE, 8, LANES), f32),
-            pltpu.VMEM((SIDE, 8, LANES), f32),
-            pltpu.VMEM((ZERO, 8, LANES), f32),
-            pltpu.VMEM((ZERO, 8, LANES), f32),
+            pltpu.VMEM((SIDE, 8, LANES), bf16),
+            pltpu.VMEM((SIDE, 8, LANES), bf16),
+            pltpu.VMEM((2, 8, LANES), bf16),
+            pltpu.VMEM((ZERO, 8, LANES), bf16),
             pltpu.VMEM((lines, LANES), f32),
             dma((6, LOADS)),
             dma((2,)),
+            dma(()),
+            dma(()),
             dma(()),
             dma(()),
             dma(()),

time: 95.1 us -> 92.4 us (0.972)
  Pallas kernels: 94.4 us -> 91.7 us
    pallas_call x1, Pallas kernels: 90.2 us -> 87.5 us  [local(): pl.pallas_call(kernel, out_shape=(pltpu.VMEM((n, ZERO * d), bf16), pltpu....]
where the time goes in v4:
time: 92.4 us; the launch traced here: 92.3 us
  Pallas kernels  91.7 us (99%)
    pallas_call x1, Pallas kernels, local(): pl.pallas_call(kernel, out_shape=(pltpu.VMEM((n, ZERO * d), bf16), pltpu....  87.5 us
    pallas_call x1, Pallas kernels, local(): pl.pallas_call(writer, out_shape=(pltpu.HBM((n, ZERO * d), bf16), pltpu.H...  4.23 us

profile of v4, /device:TPU:1, one launch (start us, length us, event | category | flops | bytes accessed | tf_op | source)
XLA Modules:
  0.0 92.3 jit_solution(2665116364752091942)
XLA Ops:
  0.6 87.5 %update_gather.1 = (bf16[432,5120]{1,0:T(8,128)(2,1)S(1)}, bf16[432,5120]{1,0:T(8,128)(2,1)S(1)}, f32[432,640]{1,0:T(8,128)S(1)}, f32[432,640]{1,0:T(8,128)S(1)}...) custom-call(f32[432,640]{1,0:T(8,128)} %bitcast.15, f32[432,640]{1,0:T(8,128)} %bitcast.16, ...), custom_call_target="tpu_custom_call" | custom-call | tf_op jit(solution)/shard_map/update_gather/pallas_call | solution.py:297
  88.1 4.2 %write_out.1 = (bf16[432,5120]{1,0:T(8,128)(2,1)}, bf16[432,5120]{1,0:T(8,128)(2,1)}, f32[1,432]{1,0:T(1,128)}, f32[1,432]{1,0:T(1,128)}, bf16[40,128]{1,0:T(8,1...) custom-call(bf16[432,5120]{1,0:T(8,128)(2,1)S(1)} %get-tuple-element.21.rg, ...), custom_call_target="tpu_custom_call" | custom-call | tf_op jit(solution)/shard_map/write_out/pallas_call | solution.py:343

commit v5 on v4

v5 whole, which is shorter than its diff:
```python
import functools

import jax
import jax.numpy as jnp
from jax import lax
from jax.experimental import pallas as pl
from jax.experimental.pallas import tpu as pltpu
from jax.sharding import PartitionSpec as P

learn_rate = 0.25
hold_rate = 0.8

LANES = 128
CHUNK = 48
AHEAD = 6
SOONER = 6
LOADS = 3
WRITES = 4
ZERO, MODEL, SIDE = 8, 32, 4

f32, bf16 = jnp.float32, jnp.bfloat16


def iota(shape, dim):
    return lax.broadcasted_iota(jnp.int32, shape, dim)


def other_core(z):
    return z + 1 - 2 * lax.rem(z, 2)


def at_zero(z):
    return {"zero": lax.rem(z, ZERO), "model": lax.axis_index("model")}


def remote(src, dst, send, recv, to):
    return pltpu.make_async_remote_copy(
        src_ref=src, dst_ref=dst, send_sem=send, recv_sem=recv, device_id=to,
        device_id_type=pl.DeviceIdType.MESH,
    )


def bytes_of(ref, sem):
    pltpu.make_async_copy(ref, ref, sem).wait()


def lines_of(k):
    at = iota((CHUNK, LANES), 0) + k * CHUNK - iota((CHUNK, LANES), 1)
    return [(r, at == r * LANES) for r in range(k * CHUNK // LANES, ((k + 1) * CHUNK - 1) // LANES + 1)]


def goes_right(a, k):
    return (a + k) % 2 == 0


def exchange(items, gathered, latest, most, wide_n, sems, raw=None, early_send=None, beside_step=None):
    send_sem, fwd_send, own_recv, fwd_recv, d2d_send, d2d_recv = sems
    zero = lax.axis_index("zero")
    right, left = lax.rem(zero + 2, ZERO), lax.rem(zero + 6, ZERO)
    far, mate = lax.rem(zero + 4, ZERO), other_core(zero)
    groups = [it for it in items if goes_right(*it)], [it for it in items if not goes_right(*it)]
    orders = groups[0] + groups[1], groups[1] + groups[0]
    early = 0 if raw is None else 1
    n = len(items)

    def part_of(item, z):
        a, k = item
        columns = pl.ds(pl.multiple_of(z * wide_n, LANES), wide_n)
        return gathered[a].at[pl.ds(k * CHUNK, CHUNK), columns]

    def rows_wait(rows, sem):
        ref = next(g for g in gathered if g is not None)
        blocks = next(b for b in range(1, ZERO + 1) if rows % (8 * b) == 0 and rows // b <= ref.shape[0])
        bytes_of(ref.at[pl.ds(0, rows // blocks), pl.ds(0, blocks * wide_n)], sem)

    rates = {}

    def rate_of(item):
        if item not in rates:
            a, k = item
            top = None
            for r, mine in lines_of(k):
                line = jnp.broadcast_to(most[a * 4 + r : a * 4 + r + 1], (CHUNK, LANES))
                part = jnp.max(jnp.where(mine, line, 0.0), axis=1, keepdims=True)
                top = part if top is None else jnp.maximum(top, part)
            rates[item] = 1.0 / top
        return rates[item]

    def keep(item, z, values):
        a, k = item
        columns = pl.ds(pl.multiple_of(z * wide_n, LANES), wide_n)
        gathered[a][k * CHUNK : (k + 1) * CHUNK, columns] = (values * rate_of(item)).astype(bf16)

    def push(item, z):
        ref = part_of(item, z)
        remote(ref, ref, d2d_send, d2d_recv, at_zero(mate)).start()

    ready = set()

    def send_own(i):
        fresh = [it for it in dict.fromkeys((orders[0][i], orders[1][i])) if it not in ready]
        for a, k in fresh:
            keep((a, k), zero, latest[a][k * CHUNK : (k + 1) * CHUNK, :])
            ready.add((a, k))
        if i >= early:
            for way, to in enumerate((right, left)):
                ref = part_of(orders[way][i], zero)
                remote(ref, ref, send_sem.at[way], own_recv.at[way, i], at_zero(to)).start()
        for item in fresh:
            push(item, zero)

    def arrive(way, i):
        item, origin = orders[way][i], (left, right)[way]
        ref = part_of(item, origin)
        if i < early:
            bytes_of(raw.at[way], own_recv.at[way, i])
            keep(item, origin, raw[way])
        else:
            remote(ref, ref, send_sem.at[way], own_recv.at[way, i], at_zero(origin)).wait_recv()
        if i < len(groups[way]):
            to = (right, left)[way]
            remote(ref, ref, fwd_send.at[way], fwd_recv.at[way, i], at_zero(to)).start()
        push(item, origin)

    def arrive_far(i):
        for way in range(2):
            if i < len(groups[way]):
                ref = part_of(groups[way][i], far)
                remote(ref, ref, fwd_send.at[way], fwd_recv.at[way, i], at_zero(far)).wait_recv()
                push(groups[way][i], far)

    most_far = max(len(g) for g in groups)
    for i in range(min(AHEAD, n)):
        send_own(i)
    far_done = 0
    for i in range(n):
        for way in range(2):
            arrive(way, i)
        if i + AHEAD < n:
            send_own(i + AHEAD)
        if i > AHEAD and far_done < most_far:
            arrive_far(far_done)
            far_done += 1
        if beside_step is not None:
            beside_step(i, n)
    for i in range(far_done, most_far):
        arrive_far(i)

    for way in range(2):
        rows_wait((n - early) * CHUNK, send_sem.at[way])
        if groups[way]:
            rows_wait(len(groups[way]) * CHUNK, fwd_send.at[way])
    if early:
        bytes_of(raw, early_send)
    rows_wait(4 * n * CHUNK, d2d_send)
    rows_wait(4 * n * CHUNK, d2d_recv)


def kernel(
    wg, fg, sg, wu, fu, su, nt, ns,
    rg, ru, lg, lu, cg, cu, norm, most_ref,
    stage, raw, peak, nin, mx, n1, n2, n3, nz, wide,
    in_sem, nin_sem, mx_send, mx_recv, n_send, n1_recv, n2_recv, n3_recv, nz_recv, nm_recv,
    early_send, *sems,
):
    zero, model = lax.axis_index("zero"), lax.axis_index("model")
    rows_n, wide_n = lg.shape
    pieces = rows_n // CHUNK
    gathered, latest = (rg, ru), (lg, lu)

    right, left = lax.rem(zero + 2, ZERO), lax.rem(zero + 6, ZERO)
    far = lax.rem(zero + 4, ZERO)
    mate = zero + 1 - 2 * lax.rem(zero, 2)
    x, y = lax.rem(model, SIDE), lax.rem(lax.div(model, SIDE), SIDE)
    beside = {"zero": zero, "model": lax.rem(model + MODEL // 2, MODEL)}

    def at_x(j):
        return {"zero": zero, "model": model - x + lax.rem(x + j, SIDE)}

    def at_y(j):
        return {"zero": zero, "model": model + (lax.rem(y + j, SIDE) - y) * SIDE}

    barrier = pltpu.get_barrier_semaphore()
    for j in range(1, ZERO):
        pl.semaphore_signal(barrier, inc=1, device_id=at_zero(zero + j))
    for j in range(1, SIDE):
        pl.semaphore_signal(barrier, inc=1, device_id=at_x(j))
        pl.semaphore_signal(barrier, inc=1, device_id=at_y(j))

    pl.semaphore_signal(barrier, inc=1, device_id=beside)

    loads = {}
    some = rows_n // LOADS
    for k in range(LOADS):
        for a, group in enumerate(((wg, fg, sg), (wu, fu, su))):
            for i, ref in enumerate(group):
                rows = pl.ds(k * some, some)
                loads[a, k, i] = pltpu.make_async_copy(
                    ref.at[rows], stage.at[a * 3 + i, rows], in_sem.at[a * 3 + i, k]
                )
                loads[a, k, i].start()
    norm_loads = [
        pltpu.make_async_copy(ref, nin.at[pl.ds(i, 1)], nin_sem.at[i])
        for i, ref in enumerate((nt, ns))
    ]
    for c in norm_loads:
        c.start()

    for k in range(pieces):
        rows = slice(k * CHUNK, (k + 1) * CHUNK)
        for a in range(2):
            if k * CHUNK % some == 0:
                for i in range(3):
                    loads[a, k * CHUNK // some, i].wait()
            w, first, second = (stage[a * 3 + i, rows, :] for i in range(3))
            hold = hold_rate * first + second
            new = w - learn_rate * hold
            latest[a][rows, :] = new
            size = jnp.abs(new)
            tall = size[:, :LANES]
            for at in range(LANES, wide_n, LANES):
                tall = jnp.maximum(tall, size[:, at : at + LANES])
            peak[a, rows, :] = tall
    best = [None] * 8
    for k in range(pieces):
        for a in range(2):
            top = jnp.max(peak[a, k * CHUNK : (k + 1) * CHUNK, :], axis=1, keepdims=True)
            at = iota((CHUNK, LANES), 0) + k * CHUNK - iota((CHUNK, LANES), 1)
            for r in range(k * CHUNK // LANES, ((k + 1) * CHUNK - 1) // LANES + 1):
                line = jnp.max(jnp.where(at == r * LANES, top, 0.0), axis=0, keepdims=True)
                old = best[a * 4 + r]
                best[a * 4 + r] = line if old is None else jnp.maximum(old, line)
    for r in range(8):
        mx[zero, pl.ds(r, 1), :] = best[r]

    for c in norm_loads:
        c.wait()
    part = jnp.concatenate(
        [nin[0:1, :] + nin[1:2, :], jnp.zeros((1, LANES - nin.shape[1]), f32)], axis=1
    ).astype(bf16).astype(f32)
    width = nin.shape[1]
    begin = model * width
    lane0 = lax.rem(begin, LANES)
    turned = pltpu.roll(jnp.broadcast_to(part, (8, LANES)), lane0, 1)
    place = iota((8, LANES), 0) * LANES + iota((8, LANES), 1) - begin
    n1[x] = jnp.where((place >= 0) & (place < width), turned, 0.0).astype(bf16)

    pl.semaphore_wait(barrier, ZERO + 2 * (SIDE - 1))

    for j in (4, 5, 3, 6, 2, 7, 1):
        remote(mx.at[zero], mx.at[zero], mx_send, mx_recv, at_zero(zero + j)).start()
    for way, to in enumerate((right, left)):
        rows = pl.ds(way * CHUNK, CHUNK)
        remote(lg.at[rows], raw.at[way], early_send, sems[2].at[way, 0], at_zero(to)).start()
    for j in range(1, SIDE):
        remote(n1.at[x], n1.at[x], n_send, n1_recv, at_x(j)).start()

    bytes_of(mx.at[pl.ds(0, ZERO - 1)], mx_recv)
    bytes_of(mx.at[pl.ds(0, ZERO - 1)], mx_send)
    most = jnp.max(mx[...], axis=0)
    most_ref[...] = most
    for r in range(4):
        some = min(LANES, rows_n - r * LANES)
        cg[:, r * LANES : r * LANES + some] = most[r : r + 1, :some]
        cu[:, r * LANES : r * LANES + some] = most[4 + r : 5 + r, :some]

    def gain_step(i, n):
        marks = [n * v // 18 for v in (0, 2, 5, 9, 14)]
        if i == marks[0]:
            bytes_of(n1.at[pl.ds(0, SIDE - 1)], n1_recv)
            bytes_of(n1.at[pl.ds(0, SIDE - 1)], n_send)
            n2[y] = jnp.sum(n1[...].astype(f32), axis=0).astype(bf16)
            for j in range(1, SIDE):
                remote(n2.at[y], n2.at[y], n_send, n2_recv, at_y(j)).start()
        if i == marks[1]:
            bytes_of(n2.at[pl.ds(0, SIDE - 1)], n2_recv)
            bytes_of(n2.at[pl.ds(0, SIDE - 1)], n_send)
            n3[0] = jnp.sum(n2[...].astype(f32), axis=0).astype(bf16)
            remote(n3.at[0], n3.at[1], n_send, n3_recv, beside).start()
        if i == marks[2]:
            bytes_of(n3.at[1], n3_recv)
            bytes_of(n3.at[0], n_send)
            nz[zero] = jnp.sum(n3[...].astype(f32), axis=0).astype(bf16)
            for z in (far, left, right):
                remote(nz.at[zero], nz.at[zero], n_send, nz_recv, at_zero(z)).start()
        if i == marks[3]:
            bytes_of(nz.at[pl.ds(0, 3)], nz_recv)
            bytes_of(nz.at[pl.ds(0, 3)], n_send)
            for z in (zero, far, left, right):
                remote(nz.at[z], nz.at[z], n_send, nm_recv, at_zero(mate)).start()
        if i == marks[4]:
            bytes_of(nz.at[pl.ds(0, 4)], nm_recv)
            bytes_of(nz.at[pl.ds(0, 4)], n_send)
            for z in range(ZERO):
                wide[z * 5 : z * 5 + 5, :] = nz[z].astype(f32)[0:5]
            norm[...] = wide[...].astype(bf16)

    gates = [(0, k) for k in range(pieces)]
    for odd, items in enumerate((gates, gates + [(1, k) for k in range(SOONER)])):

        @pl.when(lax.div(model, MODEL // 2) == odd)
        def _():
            exchange(items, gathered, latest, most, wide_n, sems, raw, early_send, gain_step)


def later_kernel(lu, most_ref, ru, *sems):
    zero, model = lax.axis_index("zero"), lax.axis_index("model")
    rows_n, wide_n = lu.shape
    barrier = pltpu.get_barrier_semaphore()
    for z in (zero + 2, zero + 6, other_core(zero)):
        pl.semaphore_signal(barrier, inc=1, device_id=at_zero(z))
    pl.semaphore_wait(barrier, 3)
    most = most_ref[...]
    ups = [(1, k) for k in range(rows_n // CHUNK)]
    for odd, items in enumerate((ups, ups[SOONER:])):

        @pl.when(lax.div(model, MODEL // 2) == odd)
        def _():
            exchange(items, (None, ru), (None, lu), most, wide_n, sems)


def write(pairs, sems):
    copies = []
    for src, dst, parts in pairs:
        n = src.shape[0]
        step = n if parts == 1 else -(-n // parts // 8) * 8
        for at in range(0, n, step):
            rows = pl.ds(at, min(step, n - at))
            whole = parts == 1
            copies.append(
                pltpu.make_async_copy(
                    src if whole else src.at[rows], dst if whole else dst.at[rows], sems.at[len(copies)]
                )
            )
            copies[-1].start()
    for c in copies:
        c.wait()


def writer(rg, lg, lu, cg, cu, norm, rg_o, cg_o, cu_o, norm_o, lg_o, lu_o, sems):
    write(
        [(rg, rg_o, WRITES), (lg, lg_o, 1), (lu, lu_o, 1), (cg, cg_o, 1), (cu, cu_o, 1), (norm, norm_o, 1)],
        sems,
    )


def later_writer(sooner, later, ru_o, sems):
    n = later.shape[0]
    cut = SOONER * CHUNK
    for odd in range(2):

        @pl.when(lax.div(lax.axis_index("model"), MODEL // 2) == odd)
        def _():
            if odd:
                pairs = [(sooner.at[pl.ds(0, cut)], ru_o.at[pl.ds(0, cut)], WRITES)]
                pairs.append((later.at[pl.ds(cut, n - cut)], ru_o.at[pl.ds(cut, n - cut)], 2))
            else:
                pairs = [(later, ru_o, WRITES)]
            write(pairs, sems)


def local(w_gate, first_gate, second_gate, w_up, first_up, second_up, norm_train, norm_step):
    weights = [v.T for v in (w_gate, first_gate, second_gate, w_up, first_up, second_up)]
    n, d = weights[0].shape
    small = norm_train.shape[0]
    pieces = n // CHUNK
    lines = ZERO * MODEL * small // LANES
    vmem, hbm = pl.BlockSpec(memory_space=pltpu.VMEM), pl.BlockSpec(memory_space=pltpu.HBM)
    dma = pltpu.SemaphoreType.DMA
    limit, low = 48 * 1024 * 1024, 8 * 1024 * 1024

    def in_vmem(*values):
        return [pltpu.with_memory_space_constraint(v, pltpu.VMEM) for v in values]

    def sems_for(count):
        return [dma((2,)), dma((2,)), dma((2, count)), dma((2, count)), dma(()), dma(())]

    rg, sooner, lg, lu, cg, cu, norm, most = pl.pallas_call(
        kernel,
        out_shape=(
            pltpu.VMEM((n, ZERO * d), bf16),
            pltpu.VMEM((n, ZERO * d), bf16),
            pltpu.VMEM((n, d), f32),
            pltpu.VMEM((n, d), f32),
            pltpu.VMEM((1, n), f32),
            pltpu.VMEM((1, n), f32),
            pltpu.VMEM((lines, LANES), bf16),
            pltpu.VMEM((8, LANES), f32),
        ),
        in_specs=[hbm] * 8,
        out_specs=(vmem,) * 8,
        scratch_shapes=[
            pltpu.VMEM((6, n, d), f32),
            pltpu.VMEM((2, CHUNK, d), f32),
            pltpu.VMEM((2, n, LANES), f32),
            pltpu.VMEM((2, small), f32),
            pltpu.VMEM((ZERO, 8, LANES), f32),
            pltpu.VMEM((SIDE, 8, LANES), bf16),
            pltpu.VMEM((SIDE, 8, LANES), bf16),
            pltpu.VMEM((2, 8, LANES), bf16),
            pltpu.VMEM((ZERO, 8, LANES), bf16),
            pltpu.VMEM((lines, LANES), f32),
            dma((6, LOADS)),
            dma((2,)),
            *[dma(())] * 9,
            *sems_for(pieces + SOONER),
        ],
        compiler_params=pltpu.CompilerParams(
            collective_id=0, has_side_effects=True, vmem_limit_bytes=limit
        ),
        name="update_gather",
    )(*weights, norm_train.reshape(1, small), norm_step.reshape(1, small))
    rg, cg, cu, norm, lg_o, lu_o = pl.pallas_call(
        writer,
        out_shape=(
            pltpu.HBM((n, ZERO * d), bf16),
            pltpu.HBM((1, n), f32),
            pltpu.HBM((1, n), f32),
            pltpu.HBM((lines, LANES), bf16),
            pltpu.HBM((n, d), f32),
            pltpu.HBM((n, d), f32),
        ),
        in_specs=[vmem] * 6,
        out_specs=(hbm,) * 6,
        scratch_shapes=[dma((WRITES + 5,))],
        compiler_params=pltpu.CompilerParams(has_side_effects=True, vmem_limit_bytes=low),
        name="write_out",
    )(*in_vmem(rg, lg, lu, cg, cu, norm))
    most, rg = lax.optimization_barrier((most, rg))
    later = pl.pallas_call(
        later_kernel,
        out_shape=pltpu.VMEM((n, ZERO * d), bf16),
        in_specs=[vmem] * 2,
        out_specs=vmem,
        scratch_shapes=sems_for(pieces),
        compiler_params=pltpu.CompilerParams(
            collective_id=1, has_side_effects=True, vmem_limit_bytes=low
        ),
        name="later_gather",
    )(*in_vmem(lu, most))
    ru = pl.pallas_call(
        later_writer,
        out_shape=pltpu.HBM((n, ZERO * d), bf16),
        in_specs=[vmem] * 2,
        out_specs=hbm,
        scratch_shapes=[dma((WRITES + 2,))],
        compiler_params=pltpu.CompilerParams(vmem_limit_bytes=low),
        name="write_later",
    )(*in_vmem(sooner, later))
    return rg.T, ru.T, cg.reshape(-1), cu.reshape(-1), norm.reshape(-1), lg_o.T, lu_o.T


def solution(mesh):
    return jax.shard_map(
        local,
        mesh=mesh,
        in_specs=(P("zero", "model"),) * 6 + (P(("zero", "model")),) * 2,
        out_specs=(
            P(None, "model"),
            P(None, "model"),
            P("model"),
            P("model"),
            P(),
            P("zero", "model"),
            P("zero", "model"),
        ),
        check_vma=False,
    )
```

time: 92.4 us -> 91.5 us (level)
  the two profiles are of different devices: /device:TPU:1 before, /device:TPU:33 now
where the time goes in v5:
time: 91.5 us; the launch traced here: 91.4 us
  Pallas kernels  90.8 us (99%)
    pallas_call x1, Pallas kernels, local(): pl.pallas_call(kernel, out_shape=(pltpu.VMEM((n, ZERO * d), bf16), pltpu....  64.2 us
    pallas_call x1, Pallas kernels, local(): pl.pallas_call(later_kernel, out_shape=pltpu.VMEM((n, ZERO * d), bf16), i...  21.5 us
    pallas_call x1, Pallas kernels, local(): pl.pallas_call(writer, out_shape=(pltpu.HBM((n, ZERO * d), bf16), pltpu.H...  2.87 us
    pallas_call x1, Pallas kernels, local(): pl.pallas_call(later_writer, out_shape=pltpu.HBM((n, ZERO * d), bf16), in...  2.15 us

profile of v5, /device:TPU:33, one launch (start us, length us, event | category | flops | bytes accessed | tf_op | source)
XLA Modules:
  0.0 91.4 jit_solution(4020692736357146463)
XLA Ops:
  0.6 64.2 %update_gather.1 = (bf16[432,5120]{1,0:T(8,128)(2,1)S(1)}, bf16[432,5120]{1,0:T(8,128)(2,1)S(1)}, f32[432,640]{1,0:T(8,128)S(1)}, f32[432,640]{1,0:T(8,128)S(1)}...) custom-call(f32[432,640]{1,0:T(8,128)} %bitcast.16, ...), custom_call_target="tpu_custom_call" | custom-call | tf_op jit(solution)/shard_map/update_gather/pallas_call | solution.py:378
  64.9 2.9 %write_out.1 = (bf16[432,5120]{1,0:T(8,128)(2,1)}, f32[1,432]{1,0:T(1,128)}, f32[1,432]{1,0:T(1,128)}, bf16[40,128]{1,0:T(8,128)(2,1)}, f32[432,640]{1,0:T(8,128)}, /*index=5*/f32[432,640]{1,0:T(8,128)}) custom-call(bf16[432,5120]{1,0:T(8,128)(2,1)S(1)} %get-tuple-element.24.rg, f32[432,640]{1,0:T(8,128)S(1)} %get-tuple-element.25.lg, ...), custom_call_target="tpu_custom_call" | custom-call | tf_op jit(solution)/shard_map/write_out/pallas_call | solution.py:413
  67.7 21.5 %later_gather.1.later = bf16[432,5120]{1,0:T(8,128)(2,1)S(1)} custom-call(f32[432,640]{1,0:T(8,128)S(1)} %get-tuple-element.26.lu, f32[8,128]{1,0:T(8,128)S(1)} %get-tuple-element.33.most_ref), custom_call_target="tpu_custom_call" | custom-call | tf_op jit(solution)/shard_map/later_gather/pallas_call | solution.py:430
  89.3 2.1 %write_later.1 = bf16[432,5120]{1,0:T(8,128)(2,1)} custom-call(bf16[432,5120]{1,0:T(8,128)(2,1)S(1)} %get-tuple-element.32.sooner, bf16[432,5120]{1,0:T(8,128)(2,1)S(1)} %later_gather.1.later), custom_call_target="tpu_custom_call" | custom-call | tf_op jit(solution)/shard_map/write_later/pallas_call | solution.py:441
